TPU v7x, 128 devices: a whole 4x4x4 slice. The times are simulated.
128 devices in a mesh: batch: 4 (over y), expert: 8 (over x, core), tensor: 4 (over z).
Axes of the slice: x: 4, y: 4, z: 4, core: 2. Of those that a mesh axis runs over, the one named last changes fastest.
Arguments:
- tokens: bfloat16 [8, 1024, 4096], P('expert', 'batch', 'tensor'), may hold values from -8 to 8
- gain: bfloat16 [4096], P('tensor'), may hold values from 0.5 to 1.5
- phi: bfloat16 [4096, 512], P('tensor'), may hold values from -1 to 1
- w_gate: bfloat16 [8, 4096, 14336], P('expert', None, ('batch', 'tensor')), may hold values from -0.125 to 0.125
- w_up: bfloat16 [8, 4096, 14336], P('expert', None, ('batch', 'tensor')), may hold values from -0.125 to 0.125
- w_down: bfloat16 [8, 14336, 4096], P('expert', ('batch', 'tensor')), may hold values from -0.09375 to 0.09375
Outputs:
- moe_out: bfloat16 [8, 1024, 4096], P('expert', 'batch', 'tensor')
All inputs are finite; a program needn't handle non-finite values.
Results may differ from a plain program's by a relative error of at most 0.025.
Values may be sent and summed in bfloat16 or wider, within the bound.
A program may use at most 128 MiB of HBM per device.

v0:
```python
import jax
import jax.numpy as jnp
from jax import lax
from jax.sharding import PartitionSpec as P

D = 4096
P_SIZE = 64


def sent_to_all(x, axis):
    size = lax.axis_size(axis)
    return lax.all_to_all(jnp.broadcast_to(x[None], (size, *x.shape)), axis, 0, 0, tiled=True)


def of_everyone(x, axis):
    return sent_to_all(x, axis).sum(axis=0)


def packed_total(arrays, axis):
    ends = [0]
    for a in arrays:
        ends.append(ends[-1] + a.size)
    running = of_everyone(jnp.concatenate([a.ravel() for a in arrays]), axis)
    return tuple((running[b:e].reshape(a.shape) for a, b, e in zip(arrays, ends, ends[1:])))


def collected_together(x, axis):
    leaves = jax.tree.leaves(x)
    order = sorted(range(len(leaves)), key=lambda k: -leaves[k].size)
    width = (1, *leaves[order[0]].shape)[-1]
    lines = [
        jnp.pad(leaves[k].reshape(-1), (0, -leaves[k].size % width)).reshape(-1, width)
        for k in order
    ]
    both, at, found = (sent_to_all(jnp.concatenate(lines), axis), 0, {})
    for k, line in zip(order, lines):
        piece = both[:, at : at + len(line)].reshape(len(both), -1)
        found[k] = piece[:, : leaves[k].size].reshape(-1, *leaves[k].shape)
        at += len(line)
    numbers = iter(range(len(leaves)))
    return jax.tree.map(lambda _: found[next(numbers)], x)


def combined_pairwise(pieces, combine):
    while len(jax.tree.leaves(pieces)[0]) > 1:
        pieces = jax.vmap(combine)(
            *(jax.tree.map(lambda part: part[side::2], pieces) for side in (0, 1))
        )
    return jax.tree.map(lambda part: part[0], pieces)


def joined_all(x, axis, combine):
    pieces = collected_together(x, axis)
    return combined_pairwise(pieces, combine)


def cut_along(x, dim, size):
    dims = x.shape
    parts = x.reshape(*dims[:dim], size, dims[dim] // size, *dims[dim + 1 :])
    return jnp.moveaxis(parts, dim, 0)


def summed_on_arrival(x, axis, dim):
    size = lax.axis_size(axis)
    parts = lax.all_to_all(cut_along(x, dim, size), axis, 0, 0, tiled=True)
    return jnp.sum(parts.astype(jnp.float32), axis=0)


def laid_out(parts, dim):
    dims = list(parts.shape[1:])
    dims[dim] *= parts.shape[0]
    return jnp.moveaxis(parts, 0, dim).reshape(dims)


def collect(x, axis, dim):
    parts = sent_to_all(x, axis)
    return laid_out(parts, dim)


def joint_totals(left_pair, right_pair):
    new_max = jnp.maximum(left_pair[0], right_pair[0])
    merged = left_pair[1] * jnp.exp(left_pair[0] - new_max) + right_pair[1] * jnp.exp(
        right_pair[0] - new_max
    )
    return (new_max, merged)


def local(tokens, gain, phi, w_gate, w_up, w_down):
    tokens_f = tokens[0].astype(jnp.float32)
    gain_f = gain.astype(jnp.float32)
    scaled = (tokens_f * gain_f[None, :]).astype(jnp.bfloat16)
    squares = jnp.sum(tokens_f * tokens_f, axis=1)
    partial_logits = jnp.dot(scaled, phi, preferred_element_type=jnp.float32)
    squares, partial_logits = packed_total((squares, partial_logits), "tensor")
    inv_rms = lax.rsqrt(squares / D + 1e-06)
    logits = partial_logits * inv_rms[:, None]
    normed = (tokens_f * gain_f[None, :] * inv_rms[:, None]).astype(jnp.bfloat16)
    combine = jax.nn.softmax(logits, axis=1).astype(jnp.bfloat16)
    local_max = jnp.max(logits, axis=0)
    local_total = jnp.sum(jnp.exp(logits - local_max[None, :]), axis=0)
    column_max, column_total = joined_all((local_max, local_total), "batch", joint_totals)
    dispatch = (jnp.exp(logits - column_max[None, :]) / column_total[None, :]).astype(jnp.bfloat16)
    slot_partial = jnp.einsum("ts,td->sd", dispatch, normed, preferred_element_type=jnp.float32)
    per_device = w_gate.shape[0]
    experts = phi.shape[1] // P_SIZE
    width_share = tokens.shape[2]
    slot_partial = slot_partial.reshape(experts, P_SIZE, width_share)
    quarter = summed_on_arrival(slot_partial.astype(jnp.bfloat16), "batch", 1).astype(jnp.bfloat16)
    exchanged = lax.all_to_all(quarter, "expert", split_axis=0, concat_axis=0, tiled=True)
    arrived = collect(exchanged, "batch", 1)
    groups = arrived.shape[0] // per_device
    arrived = arrived.reshape(groups, per_device, P_SIZE, width_share)
    hidden_share = w_gate.shape[2]
    shard_piece = lax.all_gather(arrived, "tensor", axis=3, tiled=True)
    gate_next = jnp.einsum(
        "gxpd,xdf->gxpf", shard_piece, w_gate, preferred_element_type=jnp.float32
    )
    up_next = jnp.einsum("gxpd,xdf->gxpf", shard_piece, w_up, preferred_element_type=jnp.float32)
    hidden = (jax.nn.silu(gate_next) * up_next).astype(jnp.bfloat16)
    batch_count = lax.axis_size("batch")
    tensor_count = lax.axis_size("tensor")
    hidden = hidden.reshape(groups, per_device, batch_count, P_SIZE // batch_count, hidden_share)
    down_split = w_down.reshape(per_device, hidden_share, tensor_count, D // tensor_count)
    partials = jnp.einsum(
        "gxbqf,xftd->btgxqd", hidden, down_split, preferred_element_type=jnp.float32
    )
    partials = partials.reshape(
        batch_count * tensor_count, groups, per_device, P_SIZE // batch_count, width_share
    ).astype(jnp.bfloat16)
    summed = summed_on_arrival(partials, ("batch", "tensor"), 0)
    slot_out = summed[0].astype(jnp.bfloat16)
    returned = lax.all_to_all(slot_out, "expert", split_axis=0, concat_axis=0, tiled=True)
    returned = returned.reshape(experts, P_SIZE // batch_count, width_share)
    returned = collect(returned, "batch", 1)
    moe_out = jnp.dot(
        combine, returned.reshape(experts * P_SIZE, width_share), preferred_element_type=jnp.float32
    )
    return moe_out.astype(jnp.bfloat16)[None]


def solution(mesh):
    placed = (
        P("expert", "batch", "tensor"),
        P("tensor"),
        P("tensor", None),
        P("expert", None, ("batch", "tensor")),
        P("expert", None, ("batch", "tensor")),
        P("expert", ("batch", "tensor"), None),
    )
    return jax.shard_map(
        local, mesh=mesh, in_specs=placed, out_specs=P("expert", "batch", "tensor"), check_vma=False
    )
```

profile of v0, /device:TPU:0, one launch (start us, length us, event | category | flops | bytes accessed | tf_op | source)
XLA Modules:
  0.0 282.4 jit_solution(13784396119925911884)
XLA Ops:
  6.5 0.0 copy-start
  6.5 0.0 all-gather.2.cloned.1.call-start
  6.5 1.3 fusion.22
  7.9 0.7 convert_element_type.86
  8.5 0.0 copy-done
  8.5 1.5 convolution_bitcast_fusion
  10.0 0.1 copy.46
  10.2 2.5 broadcast_in_dim.12
  12.8 31.6 %all_to_all.41 = f32[4,1,131328]{2,1,0:T(1,128)S(1)} all-to-all(f32[4,1,131328]{2,1,0:T(1,128)S(1)} %broadcast_in_dim.12), channel_id=1, replica_groups=mesh['batch'=4,'expert'=8,'tensor'=4] {'tensor'}, dimensions={0} | all-to-all | bytes 4202496 | tf_op jit(solution)/shard_map/all_to_all | solution.py:12
  44.4 0.0 copy-start.2
  44.4 10.6 %reduce_sum.61 = f32[131328]{0:T(1024)} reduce(f32[4,1,131328]{2,1,0:T(1,128)S(1)} %all_to_all.41, f32[]{:T(128)} %constant.6.clone.1), dimensions={0,1}, to_apply=%region_1.0 | reduce | flops 393984 | bytes 2626564 | tf_op jit(solution)/shard_map/reduce_sum | solution.py:16
  55.0 0.7 fusion.35
  55.7 1.1 slice.52
  56.7 0.1 reshape.121
  56.8 0.2 multiply_reduce_fusion
  57.0 0.3 exponential_reduce_fusion
  57.4 9.6 %all_to_all.42 = f32[4,2,512]{2,1,0:T(2,128)S(1)} all-to-all(f32[4,2,512]{2,1,0:T(2,128)S(1)} %broadcast_in_dim.13), channel_id=1, replica_groups=mesh['batch'=4,'expert'=8,'tensor'=4] {'batch'}, dimensions={0} | all-to-all | bytes 32768 | tf_op jit(solution)/shard_map/all_to_all | solution.py:12
  67.2 0.2 fusion.32
  67.4 0.1 copy.31
  67.5 0.0 copy-done.2
  67.5 0.5 convolution_convert_fusion
  68.0 0.1 copy.57
  68.1 15.2 %all_to_all.43 = bf16[4,8,16,1024]{3,2,1,0:T(8,128)(2,1)S(1)} all-to-all(bf16[4,8,16,1024]{3,2,1,0:T(8,128)(2,1)S(1)} %bitcast.118), channel_id=1, replica_groups=mesh['batch'=4,'expert'=8,'tensor'=4] {'batch'}, dimensions={0} | all-to-all | bytes 2097152 | tf_op jit(solution)/shard_map/all_to_all | solution.py:65
  83.3 0.2 reduce_sum.64
  83.5 11.6 %all_to_all.44 = bf16[8,16,1024]{2,1,0:T(8,128)(2,1)S(1)} all-to-all(bf16[8,16,1024]{2,1,0:T(8,128)(2,1)S(1)} %reduce_sum.64), channel_id=1, replica_groups=mesh['batch'=4,'expert'=8,'tensor'=4] {'expert'}, dimensions={0} | all-to-all | bytes 524288 | tf_op jit(solution)/shard_map/all_to_all | solution.py:109
  95.1 0.1 broadcast_in_dim.14
  95.2 17.4 %all_to_all.45 = bf16[4,8,16,1024]{3,2,1,0:T(8,128)(2,1)S(1)} all-to-all(bf16[4,8,16,1024]{3,2,1,0:T(8,128)(2,1)S(1)} %broadcast_in_dim.14), channel_id=1, replica_groups=mesh['batch'=4,'expert'=8,'tensor'=4] {'batch'}, dimensions={0} | all-to-all | bytes 2097152 | tf_op jit(solution)/shard_map/all_to_all | solution.py:12
  112.6 1.0 copy.33
  113.7 0.0 all-gather.2.cloned.1.call-update
  113.7 13.1 %reshape.131 = bf16[896,4,1024]{2,1,0:T(4,128)(2,1)} reshape(bf16[1,896,4096]{2,1,0:T(8,128)(2,1)} %param.11) | data formatting | bytes 14680064 | tf_op jit(solution)/shard_map/reshape.6
  126.8 31.1 %all-gather.2.cloned.1.call-done = bf16[8,1,64,4096]{3,2,0,1:T(8,128)(2,1)} async-done(((bf16[8,1,64,1024]{3,2,0,1:T(8,128)(2,1)}), bf16[8,1,64,4096]{3,2,0,1:T(8,128)(2,1)}) %all-gather.2.cloned.1.call-update) | async-done | bytes 4194320 | tf_op jit(solution)/shard_map/all_gather | solution.py:114
  157.9 0.0 copy-start.4
  157.9 0.0 slice-start
  157.9 10.5 %fusion.4 = f32[8,64,896]{2,1,0:T(8,128)S(1)} fusion(bf16[1,4096,896]{2,1,0:T(8,128)(2,1)} %param.9, bf16[8,1,64,4096]{3,2,0,1:T(8,128)(2,1)} %all-gather.2.cloned.1.call-done), kind=kOutput, calls=%fused_computation.4 | convolution fusion | flops 3758096384 | bytes 13369344 | tf_op jit(solution)/shard_map/gxpd,xdf->gxpf/dot_general | solution.py:115
  168.5 0.0 copy-done.4
  168.5 0.0 slice-start.1
  168.5 7.8 %fusion.11 = bf16[8,1,64,896]{3,2,0,1:T(8,128)(2,1)S(1)} fusion(f32[8,64,896]{2,1,0:T(8,128)S(1)} %fusion.4, bf16[1,4096,896]{2,1,0:T(8,128)(2,1)} %param.10, bf16[8,1,64,4096]{3,2,0,1:T(8,128)(2,1)S(1)} %copy-done.4), kind=kOutput, calls=%fused_computation.10 | convolution fusion | flops 3760848896 | bytes 14286848 | tf_op jit(solution)/shard_map/gxpd,xdf->gxpf/dot_general | solution.py:118
  176.2 0.0 slice-done
  176.2 0.0 slice-done.1
  176.3 5.6 %fusion.8 = bf16[8,4,16,4,1024]{4,2,3,1,0:T(8,128)(2,1)S(1)} fusion(bf16[8,4,16,896,1]{3,2,4,1,0:T(8,128)(2,1)S(1)} %bitcast.130, bf16[896,4,1024,1,1]{2,1,0,4,3:T(4,128)(2,1)S(1)} %bitcast.113), kind=kOutput, calls=%fused_computation.8 | convolution fusion | flops 3760193536 | bytes 12451840 | tf_op jit(solution)/shard_map/gxbqf,xftd->btgxqd/dot_general | solution.py:124
  181.9 0.4 copy.35
  182.4 56.5 %all_to_all.46 = bf16[16,1,8,1,16,1024]{5,4,2,3,1,0:T(8,128)(2,1)} all-to-all(bf16[16,1,8,1,16,1024]{5,4,2,3,1,0:T(8,128)(2,1)S(1)} %copy.35), channel_id=1, replica_groups=mesh['batch'=4,'expert'=8,'tensor'=4] {'batch','tensor'}, dimensions={0} | all-to-all | bytes 8388608 | tf_op jit(solution)/shard_map/all_to_all | solution.py:65
  238.8 3.9 %reduce_sum.65 = bf16[8,16,1024]{2,1,0:T(8,128)(2,1)} reduce(bf16[16,1,8,1,16,1024]{5,4,2,3,1,0:T(8,128)(2,1)} %all_to_all.46, bf16[]{:T(256)} %constant.15.clone.1), dimensions={0,1,3}, to_apply=%region_7.8 | reduce | flops 1966080 | bytes 4456450 | tf_op jit(solution)/shard_map/reduce_sum | solution.py:66
  242.7 0.0 copy-start.3
  242.7 4.4 %all-to-all-start.6 = ((bf16[8,1,16,1024]{3,2,1,0:T(8,128)(2,1)}), bf16[8,1,16,1024]{3,2,1,0:T(8,128)(2,1)S(1)}, u32[]{:S(2)}, u32[]{:S(2)}) async-start(bf16[8,1,16,1024]{3,2,1,0:T(8,128)(2,1)} %bitcast.35), calls=%async_computation.6 | async-start | bytes 524288 | tf_op jit(solution)/shard_map/all_to_all | solution.py:132
  247.1 0.1 broadcast_bitcast_fusion
  247.2 0.9 copy.49
  248.1 1.0 copy.48
  249.1 0.9 copy.47
  250.0 4.6 %all-to-all-done.6 = bf16[8,1,16,1024]{3,2,1,0:T(8,128)(2,1)S(1)} async-done(((bf16[8,1,16,1024]{3,2,1,0:T(8,128)(2,1)}), bf16[8,1,16,1024]{3,2,1,0:T(8,128)(2,1)S(1)}, u32[]{:S(2)}, u32[]{:S(2)}) %all-to-all-start.6) | async-done | bytes 262176 | tf_op jit(solution)/shard_map/all_to_all | solution.py:132
  254.6 0.0 copy-start.1
  254.6 1.1 broadcast_in_dim.16
  255.7 3.5 %all-to-all-start.7 = ((bf16[4,8,16,1024]{3,2,1,0:T(8,128)(2,1)}), bf16[4,8,16,1024]{3,2,1,0:T(8,128)(2,1)S(1)}, u32[]{:S(2)}, u32[]{:S(2)}) async-start(bf16[4,8,16,1024]{3,2,1,0:T(8,128)(2,1)} %broadcast_in_dim.16), calls=%async_computation.7 | async-start | bytes 2097152 | tf_op jit(solution)/shard_map/all_to_all | solution.py:12
  259.2 0.0 copy-done.3
  259.3 1.5 divide_convert_fusion.1
  260.8 0.2 convert_element_type.89
  260.9 13.3 %all-to-all-done.7 = bf16[4,8,16,1024]{3,2,1,0:T(8,128)(2,1)S(1)} async-done(((bf16[4,8,16,1024]{3,2,1,0:T(8,128)(2,1)}), bf16[4,8,16,1024]{3,2,1,0:T(8,128)(2,1)S(1)}, u32[]{:S(2)}, u32[]{:S(2)}) %all-to-all-start.7) | async-done | bytes 1048608 | tf_op jit(solution)/shard_map/all_to_all | solution.py:12
  274.2 0.1 copy.36
  274.3 1.2 fusion.21
  275.6 0.0 copy-done.1
  (12 shorter events, 0.2 us)
Async XLA Ops:
  6.5 2.0 copy-start
  6.5 151.4 %all-gather.2.cloned.1.call-start = ((), (), s32[]{:S(2)}) async-start(), calls=%async_computation.8 | async-start | bytes 5242880 | tf_op jit(solution)/shard_map/all_gather | solution.py:114
  44.4 23.1 %copy-start.2 = (bf16[1,256,1024]{2,1,0:T(8,128)(2,1)S(1)}, bf16[1,256,1024]{2,1,0:T(8,128)(2,1)}, u32[]{:S(2)}) copy-start(bf16[1,256,1024]{2,1,0:T(8,128)(2,1)} %param.6) | copy-start | bytes 1572868
  157.9 10.5 %copy-start.4 = (bf16[8,1,64,4096]{3,2,0,1:T(8,128)(2,1)S(1)}, bf16[8,1,64,4096]{3,2,0,1:T(8,128)(2,1)}, u32[]{:S(2)}) copy-start(bf16[8,1,64,4096]{3,2,0,1:T(8,128)(2,1)} %all-gather.2.cloned.1.call-done) | copy-start | bytes 12582916
  157.9 18.3 %slice-start = ((s8[7340032]{0:T(1024)(128)(4,1)}), s8[4194304]{0:T(1024)(128)(4,1)S(1)}, s32[]{:S(2)}) async-start(s8[7340032]{0:T(1024)(128)(4,1)} %bitcast.111), calls=%async_computation.9 | async-start | bytes 8388608
  168.5 7.8 %slice-start.1 = ((s8[7340032]{0:T(1024)(128)(4,1)}), s8[3145728]{0:T(1024)(128)(4,1)S(1)}, s32[]{:S(2)}) async-start(s8[7340032]{0:T(1024)(128)(4,1)} %bitcast.111), calls=%async_computation.10 | async-start | bytes 6291456
  242.7 16.5 %copy-start.3 = (f32[131328]{0:T(1024)S(1)}, f32[131328]{0:T(1024)}, u32[]{:S(2)}) copy-start(f32[131328]{0:T(1024)} %reduce_sum.61) | copy-start | bytes 1575940
  242.7 11.9 %all-to-all-start.6 = ((bf16[8,1,16,1024]{3,2,1,0:T(8,128)(2,1)}), bf16[8,1,16,1024]{3,2,1,0:T(8,128)(2,1)S(1)}, u32[]{:S(2)}, u32[]{:S(2)}) async-start(bf16[8,1,16,1024]{3,2,1,0:T(8,128)(2,1)} %bitcast.35), calls=%async_computation.6 | async-start | bytes 524288 | tf_op jit(solution)/shard_map/all_to_all | solution.py:132
  254.6 21.0 %copy-start.1 = (bf16[1024,512]{1,0:T(8,128)(2,1)S(1)}, bf16[1024,512]{1,0:T(8,128)(2,1)}, u32[]{:S(2)}) copy-start(bf16[1024,512]{1,0:T(8,128)(2,1)} %param.8) | copy-start | bytes 3145732
  255.7 18.5 %all-to-all-start.7 = ((bf16[4,8,16,1024]{3,2,1,0:T(8,128)(2,1)}), bf16[4,8,16,1024]{3,2,1,0:T(8,128)(2,1)S(1)}, u32[]{:S(2)}, u32[]{:S(2)}) async-start(bf16[4,8,16,1024]{3,2,1,0:T(8,128)(2,1)} %broadcast_in_dim.16), calls=%async_computation.7 | async-start | bytes 2097152 | tf_op jit(solution)/shard_map/all_to_all | solution.py:12
Sparse Core Ops, SparseCore 0:
  113.8 44.0 all-gather.1
where the time goes:
time: 283 us; the launch traced here: 282 us
  blocking collectives  142 us (50%)
  waiting for transfers between devices  49 us (17%)
  matrix products  27.2 us (10%)
  local copies, waits for them, and re-layouts  23.2 us (8%)
  other arithmetic  19.6 us (7%)
  between operations  13.7 us (5%)
  starting transfers between devices  7.9 us (3%)
    all_to_all x2, blocking collectives, summed_on_arrival(): parts = lax.all_to_all(cut_along(x, dim, size), axis, 0, 0, tiled=True)  71.6 us
    all_to_all x3, blocking collectives, sent_to_all(): lax.all_to_all(jnp.broadcast_to(x[None], (size, *x.shape)), axis, 0, 0, t...  58.7 us
    all_gather x1, waiting for transfers between devices, local(): shard_piece = lax.all_gather(arrived, 'tensor', axis=3, tiled=True)  31.1 us
    all_to_all x1, waiting for transfers between devices, sent_to_all(): lax.all_to_all(jnp.broadcast_to(x[None], (size, *x.shape)), axis, 0, 0, t...  13.3 us
    another operation x1, local copies, waits for them, and re-layouts  13.1 us
    all_to_all x1, blocking collectives, local(): lax.all_to_all(quarter, 'expert', split_axis=0, concat_axis=0, tiled=True)  11.6 us
    reduce_sum x1, other arithmetic, of_everyone(): return sent_to_all(x, axis).sum(axis=0)  10.6 us
    dot_general x1, matrix products, local(): jnp.einsum('gxpd,xdf->gxpf', shard_piece, w_gate, preferred_element_type=...  10.5 us
  transfers between devices with their start and end apart: 3, of which 3 were waited for; matrix products, arithmetic and copies ran while one was open for 6% of the time, Pallas kernels for 0%

commit v1 on v0

--- a/solution.py
+++ b/solution.py
@@ -5,6 +5,11 @@
 
 D = 4096
 P_SIZE = 64
+
+
+def gather_by_exchange(value, axis, dim):
+    copies = jnp.concatenate([value] * lax.axis_size(axis), axis=dim)
+    return lax.all_to_all(copies, axis, dim, dim, tiled=True)
 
 
 def sent_to_all(x, axis):
@@ -111,7 +116,7 @@
     groups = arrived.shape[0] // per_device
     arrived = arrived.reshape(groups, per_device, P_SIZE, width_share)
     hidden_share = w_gate.shape[2]
-    shard_piece = lax.all_gather(arrived, "tensor", axis=3, tiled=True)
+    shard_piece = gather_by_exchange(arrived, "tensor", 3)
     gate_next = jnp.einsum(
         "gxpd,xdf->gxpf", shard_piece, w_gate, preferred_element_type=jnp.float32
     )

time: 283 us -> 314 us (1.11)
  local copies, waits for them, and re-layouts: 23.2 us -> 60.6 us
  between operations: 13.7 us -> 0.29 us
  starting transfers between devices: 7.9 us -> 12.2 us
  blocking collectives: 142 us -> 138 us
  waiting for transfers between devices: 49 us -> 52.7 us
    all_to_all x0 -> x1, waiting for transfers between devices: none -> 34.9 us  [gather_by_exchange(): return lax.all_to_all(copies, axis, dim, dim, tiled=True)]
    all_gather x1 -> x0, waiting for transfers between devices: 31.1 us -> none  [local(): shard_piece = lax.all_gather(arrived, 'tensor', axis=3, tiled=True)]
    unnamed x19 -> x21, local copies, waits for them, and re-layouts: 3.09 us -> 21.9 us
    concatenate x0 -> x1, local copies, waits for them, and re-layouts: none -> 10.1 us  [gather_by_exchange(): copies = jnp.concatenate([value] * lax.axis_size(axis), axis=dim)]
    all_to_all x0 -> x1, local copies, waits for them, and re-layouts: none -> 9.77 us  [gather_by_exchange(): return lax.all_to_all(copies, axis, dim, dim, tiled=True)]
    all_to_all x0 -> x1, starting transfers between devices: none -> 5.12 us  [gather_by_exchange(): return lax.all_to_all(copies, axis, dim, dim, tiled=True)]
    all_to_all x2, blocking collectives: 71.6 us -> 67.6 us  [summed_on_arrival(): parts = lax.all_to_all(cut_along(x, dim, size), axis, 0, 0, tiled=True)]
where the time goes in v1:
time: 314 us; the launch traced here: 312 us
  blocking collectives  138 us (44%)
  local copies, waits for them, and re-layouts  60.6 us (19%)
  waiting for transfers between devices  52.7 us (17%)
  matrix products  26.6 us (8%)
  other arithmetic  21.8 us (7%)
  starting transfers between devices  12.2 us (4%)
    all_to_all x2, blocking collectives, summed_on_arrival(): parts = lax.all_to_all(cut_along(x, dim, size), axis, 0, 0, tiled=True)  67.6 us
    all_to_all x3, blocking collectives, sent_to_all(): lax.all_to_all(jnp.broadcast_to(x[None], (size, *x.shape)), axis, 0, 0, t...  58.7 us
    all_to_all x1, waiting for transfers between devices, gather_by_exchange(): return lax.all_to_all(copies, axis, dim, dim, tiled=True)  34.9 us
    unnamed x21, local copies, waits for them, and re-layouts  21.9 us
    all_to_all x1, waiting for transfers between devices, sent_to_all(): lax.all_to_all(jnp.broadcast_to(x[None], (size, *x.shape)), axis, 0, 0, t...  13.3 us
    another operation x1, local copies, waits for them, and re-layouts  12.8 us
    all_to_all x1, blocking collectives, local(): lax.all_to_all(quarter, 'expert', split_axis=0, concat_axis=0, tiled=True)  11.6 us
    reduce_sum x1, other arithmetic, of_everyone(): return sent_to_all(x, axis).sum(axis=0)  10.5 us
  transfers between devices with their start and end apart: 3, of which 3 were waited for; matrix products, arithmetic and copies ran while one was open for 6% of the time, Pallas kernels for 0%

profile of v1, /device:TPU:0, one launch (start us, length us, event | category | flops | bytes accessed | tf_op | source)
XLA Modules:
  0.0 311.9 jit_solution(13801155072609964513)
XLA Ops:
  0.0 0.0 copy-start
  0.0 1.3 fusion.22
  1.3 0.7 convert_element_type.86
  2.0 0.0 copy-done
  2.0 1.5 convolution_bitcast_fusion
  3.5 0.1 copy.59
  3.7 2.5 broadcast_in_dim.12
  6.2 31.6 %all_to_all.46 = f32[4,1,131328]{2,1,0:T(1,128)S(1)} all-to-all(f32[4,1,131328]{2,1,0:T(1,128)S(1)} %broadcast_in_dim.12), channel_id=1, replica_groups=mesh['batch'=4,'expert'=8,'tensor'=4] {'tensor'}, dimensions={0} | all-to-all | bytes 4202496 | tf_op jit(solution)/shard_map/all_to_all | solution.py:17
  37.8 0.0 copy-start.2
  37.9 10.5 %reduce_sum.61 = f32[131328]{0:T(1024)} reduce(f32[4,1,131328]{2,1,0:T(1,128)S(1)} %all_to_all.46, f32[]{:T(128)} %constant.6.clone.1), dimensions={0,1}, to_apply=%region_1.0 | reduce | flops 393984 | bytes 2626564 | tf_op jit(solution)/shard_map/reduce_sum | solution.py:21
  48.4 0.7 fusion.35
  49.1 1.1 slice.52
  50.2 0.1 reshape.121
  50.2 0.2 multiply_reduce_fusion
  50.4 0.3 exponential_reduce_fusion
  50.8 9.6 %all_to_all.47 = f32[4,2,512]{2,1,0:T(2,128)S(1)} all-to-all(f32[4,2,512]{2,1,0:T(2,128)S(1)} %broadcast_in_dim.13), channel_id=1, replica_groups=mesh['batch'=4,'expert'=8,'tensor'=4] {'batch'}, dimensions={0} | all-to-all | bytes 32768 | tf_op jit(solution)/shard_map/all_to_all | solution.py:17
  60.6 0.2 fusion.32
  60.8 0.1 copy.42
  60.9 0.0 copy-done.2
  60.9 0.5 convolution_convert_fusion
  61.5 0.1 copy.70
  61.5 15.2 %all_to_all.48 = bf16[4,8,16,1024]{3,2,1,0:T(8,128)(2,1)S(1)} all-to-all(bf16[4,8,16,1024]{3,2,1,0:T(8,128)(2,1)S(1)} %bitcast.123), channel_id=1, replica_groups=mesh['batch'=4,'expert'=8,'tensor'=4] {'batch'}, dimensions={0} | all-to-all | bytes 2097152 | tf_op jit(solution)/shard_map/all_to_all | solution.py:70
  76.7 0.2 reduce_sum.64
  76.9 11.6 %all_to_all.49 = bf16[8,16,1024]{2,1,0:T(8,128)(2,1)S(1)} all-to-all(bf16[8,16,1024]{2,1,0:T(8,128)(2,1)S(1)} %reduce_sum.64), channel_id=1, replica_groups=mesh['batch'=4,'expert'=8,'tensor'=4] {'expert'}, dimensions={0} | all-to-all | bytes 524288 | tf_op jit(solution)/shard_map/all_to_all | solution.py:114
  88.5 0.1 broadcast_in_dim.14
  88.6 17.4 %all_to_all.50 = bf16[4,8,16,1024]{3,2,1,0:T(8,128)(2,1)S(1)} all-to-all(bf16[4,8,16,1024]{3,2,1,0:T(8,128)(2,1)S(1)} %broadcast_in_dim.14), channel_id=1, replica_groups=mesh['batch'=4,'expert'=8,'tensor'=4] {'batch'}, dimensions={0} | all-to-all | bytes 2097152 | tf_op jit(solution)/shard_map/all_to_all | solution.py:17
  106.1 0.1 copy.44
  106.1 2.2 pad_maximum_fusion
  108.3 10.1 %copy.45 = bf16[8,1,64,4096]{2,0,1,3:T(8,128)(2,1)} copy(bf16[8,1,64,4096]{3,2,0,1:T(8,128)(2,1)} %pad_maximum_fusion) | data formatting | bytes 8388608 | tf_op jit(solution)/shard_map/concatenate | solution.py:11
  118.4 9.5 %reshape.138 = bf16[4,2,262144]{2,1,0:T(2,128)(2,1)} reshape(bf16[4096,1,8,64]{3,2,1,0:T(8,128)(2,1)} %bitcast.114) | data formatting | bytes 8388608
  128.0 5.1 %all-to-all-start.5 = ((bf16[4,2,262144]{2,1,0:T(2,128)(2,1)}), bf16[4,2,262144]{2,1,0:T(2,128)(2,1)}, u32[]{:S(2)}, u32[]{:S(2)}) async-start(bf16[4,2,262144]{2,1,0:T(2,128)(2,1)} %reshape.138), calls=%async_computation.5 | async-start | bytes 8388608 | tf_op jit(solution)/shard_map/all_to_all | solution.py:12
  133.1 12.8 %reshape.131 = bf16[896,4,1024]{2,1,0:T(4,128)(2,1)} reshape(bf16[1,896,4096]{2,1,0:T(8,128)(2,1)} %param.11) | data formatting | bytes 14680064 | tf_op jit(solution)/shard_map/reshape.6
  145.9 34.9 %all-to-all-done.5 = bf16[4,2,262144]{2,1,0:T(2,128)(2,1)} async-done(((bf16[4,2,262144]{2,1,0:T(2,128)(2,1)}), bf16[4,2,262144]{2,1,0:T(2,128)(2,1)}, u32[]{:S(2)}, u32[]{:S(2)}) %all-to-all-start.5) | async-done | bytes 4194336 | tf_op jit(solution)/shard_map/all_to_all | solution.py:12
  180.8 9.3 %reshape.139 = bf16[4096,1,8,64]{3,2,1,0:T(8,128)(2,1)} reshape(bf16[4,2,262144]{2,1,0:T(2,128)(2,1)} %all-to-all-done.5) | data formatting | bytes 8388608
  190.1 9.8 %copy.46 = bf16[8,1,64,4096]{3,2,0,1:T(8,128)(2,1)} copy(bf16[8,1,64,4096]{2,0,1,3:T(8,128)(2,1)} %bitcast.115) | data formatting | bytes 8388608 | tf_op jit(solution)/shard_map/all_to_all | solution.py:12
  199.8 0.0 copy-start.4
  199.8 0.0 slice-start
  199.8 9.9 %fusion.4 = f32[8,64,896]{2,1,0:T(8,128)S(1)} fusion(bf16[1,4096,896]{2,1,0:T(8,128)(2,1)} %param.9, bf16[8,1,64,4096]{3,2,0,1:T(8,128)(2,1)} %copy.46), kind=kOutput, calls=%fused_computation.4 | convolution fusion | flops 3758096384 | bytes 13369344 | tf_op jit(solution)/shard_map/gxpd,xdf->gxpf/dot_general | solution.py:120
  209.8 0.0 copy-done.4
  209.8 0.0 slice-start.1
  209.8 7.8 %fusion.11 = bf16[8,1,64,896]{3,2,0,1:T(8,128)(2,1)S(1)} fusion(f32[8,64,896]{2,1,0:T(8,128)S(1)} %fusion.4, bf16[1,4096,896]{2,1,0:T(8,128)(2,1)} %param.10, bf16[8,1,64,4096]{3,2,0,1:T(8,128)(2,1)S(1)} %copy-done.4), kind=kOutput, calls=%fused_computation.11 | convolution fusion | flops 3760848896 | bytes 14286848 | tf_op jit(solution)/shard_map/gxpd,xdf->gxpf/dot_general | solution.py:123
  217.6 0.0 slice-done
  217.6 0.0 slice-done.1
  217.6 5.7 %fusion.8 = bf16[8,4,16,4,1024]{4,2,3,1,0:T(8,128)(2,1)S(1)} fusion(bf16[8,4,16,896,1]{3,2,4,1,0:T(8,128)(2,1)S(1)} %bitcast.134, bf16[896,4,1024,1,1]{2,1,0,4,3:T(4,128)(2,1)S(1)} %bitcast.118), kind=kOutput, calls=%fused_computation.9 | convolution fusion | flops 3760193536 | bytes 12451840 | tf_op jit(solution)/shard_map/gxbqf,xftd->btgxqd/dot_general | solution.py:129
  223.3 0.4 copy.48
  223.7 52.4 %all_to_all.51 = bf16[16,1,8,1,16,1024]{5,4,2,3,1,0:T(8,128)(2,1)} all-to-all(bf16[16,1,8,1,16,1024]{5,4,2,3,1,0:T(8,128)(2,1)S(1)} %copy.48), channel_id=1, replica_groups=mesh['batch'=4,'expert'=8,'tensor'=4] {'batch','tensor'}, dimensions={0} | all-to-all | bytes 8388608 | tf_op jit(solution)/shard_map/all_to_all | solution.py:70
  276.1 3.9 %reduce_sum.65 = bf16[8,16,1024]{2,1,0:T(8,128)(2,1)} reduce(bf16[16,1,8,1,16,1024]{5,4,2,3,1,0:T(8,128)(2,1)} %all_to_all.51, bf16[]{:T(256)} %constant.15.clone.1), dimensions={0,1,3}, to_apply=%region_7.8 | reduce | flops 1966080 | bytes 4456450 | tf_op jit(solution)/shard_map/reduce_sum | solution.py:71
  280.0 0.0 copy-start.3
  280.0 3.5 %all-to-all-start.7 = ((bf16[8,1,16,1024]{3,2,1,0:T(8,128)(2,1)}), bf16[8,1,16,1024]{3,2,1,0:T(8,128)(2,1)S(1)}, u32[]{:S(2)}, u32[]{:S(2)}) async-start(bf16[8,1,16,1024]{3,2,1,0:T(8,128)(2,1)} %bitcast.35), calls=%async_computation.7 | async-start | bytes 524288 | tf_op jit(solution)/shard_map/all_to_all | solution.py:137
  283.5 0.1 broadcast_bitcast_fusion
  283.6 0.9 copy.62
  284.6 0.9 copy.61
  285.5 0.9 copy.60
  286.5 4.5 %all-to-all-done.7 = bf16[8,1,16,1024]{3,2,1,0:T(8,128)(2,1)S(1)} async-done(((bf16[8,1,16,1024]{3,2,1,0:T(8,128)(2,1)}), bf16[8,1,16,1024]{3,2,1,0:T(8,128)(2,1)S(1)}, u32[]{:S(2)}, u32[]{:S(2)}) %all-to-all-start.7) | async-done | bytes 262176 | tf_op jit(solution)/shard_map/all_to_all | solution.py:137
  291.0 0.0 copy-start.1
  291.0 1.1 broadcast_in_dim.16
  292.1 3.5 %all-to-all-start.8 = ((bf16[4,8,16,1024]{3,2,1,0:T(8,128)(2,1)}), bf16[4,8,16,1024]{3,2,1,0:T(8,128)(2,1)S(1)}, u32[]{:S(2)}, u32[]{:S(2)}) async-start(bf16[4,8,16,1024]{3,2,1,0:T(8,128)(2,1)} %broadcast_in_dim.16), calls=%async_computation.8 | async-start | bytes 2097152 | tf_op jit(solution)/shard_map/all_to_all | solution.py:17
  295.6 0.0 copy-done.3
  295.6 1.5 divide_convert_fusion.1
  297.1 0.2 convert_element_type.89
  297.3 13.3 %all-to-all-done.8 = bf16[4,8,16,1024]{3,2,1,0:T(8,128)(2,1)S(1)} async-done(((bf16[4,8,16,1024]{3,2,1,0:T(8,128)(2,1)}), bf16[4,8,16,1024]{3,2,1,0:T(8,128)(2,1)S(1)}, u32[]{:S(2)}, u32[]{:S(2)}) %all-to-all-start.8) | async-done | bytes 1048608 | tf_op jit(solution)/shard_map/all_to_all | solution.py:17
  310.6 0.1 copy.49
  310.7 1.2 fusion.21
  311.9 0.0 copy-done.1
  (12 shorter events, 0.2 us)
Async XLA Ops:
  0.0 2.0 copy-start
  37.8 23.1 %copy-start.2 = (bf16[1,256,1024]{2,1,0:T(8,128)(2,1)S(1)}, bf16[1,256,1024]{2,1,0:T(8,128)(2,1)}, u32[]{:S(2)}) copy-start(bf16[1,256,1024]{2,1,0:T(8,128)(2,1)} %param.6) | copy-start | bytes 1572868
  128.0 52.9 %all-to-all-start.5 = ((bf16[4,2,262144]{2,1,0:T(2,128)(2,1)}), bf16[4,2,262144]{2,1,0:T(2,128)(2,1)}, u32[]{:S(2)}, u32[]{:S(2)}) async-start(bf16[4,2,262144]{2,1,0:T(2,128)(2,1)} %reshape.138), calls=%async_computation.5 | async-start | bytes 8388608 | tf_op jit(solution)/shard_map/all_to_all | solution.py:12
  199.8 9.9 %copy-start.4 = (bf16[8,1,64,4096]{3,2,0,1:T(8,128)(2,1)S(1)}, bf16[8,1,64,4096]{3,2,0,1:T(8,128)(2,1)}, u32[]{:S(2)}) copy-start(bf16[8,1,64,4096]{3,2,0,1:T(8,128)(2,1)} %copy.46) | copy-start | bytes 12582916
  199.8 17.7 %slice-start = ((s8[7340032]{0:T(1024)(128)(4,1)}), s8[4194304]{0:T(1024)(128)(4,1)S(1)}, s32[]{:S(2)}) async-start(s8[7340032]{0:T(1024)(128)(4,1)} %bitcast.116), calls=%async_computation.9 | async-start | bytes 8388608
  209.8 7.8 %slice-start.1 = ((s8[7340032]{0:T(1024)(128)(4,1)}), s8[3145728]{0:T(1024)(128)(4,1)S(1)}, s32[]{:S(2)}) async-start(s8[7340032]{0:T(1024)(128)(4,1)} %bitcast.116), calls=%async_computation.10 | async-start | bytes 6291456
  280.0 15.6 %copy-start.3 = (f32[131328]{0:T(1024)S(1)}, f32[131328]{0:T(1024)}, u32[]{:S(2)}) copy-start(f32[131328]{0:T(1024)} %reduce_sum.61) | copy-start | bytes 1575940
  280.0 11.0 %all-to-all-start.7 = ((bf16[8,1,16,1024]{3,2,1,0:T(8,128)(2,1)}), bf16[8,1,16,1024]{3,2,1,0:T(8,128)(2,1)S(1)}, u32[]{:S(2)}, u32[]{:S(2)}) async-start(bf16[8,1,16,1024]{3,2,1,0:T(8,128)(2,1)} %bitcast.35), calls=%async_computation.7 | async-start | bytes 524288 | tf_op jit(solution)/shard_map/all_to_all | solution.py:137
  291.0 21.0 %copy-start.1 = (bf16[1024,512]{1,0:T(8,128)(2,1)S(1)}, bf16[1024,512]{1,0:T(8,128)(2,1)}, u32[]{:S(2)}) copy-start(bf16[1024,512]{1,0:T(8,128)(2,1)} %param.8) | copy-start | bytes 3145732
  292.1 18.5 %all-to-all-start.8 = ((bf16[4,8,16,1024]{3,2,1,0:T(8,128)(2,1)}), bf16[4,8,16,1024]{3,2,1,0:T(8,128)(2,1)S(1)}, u32[]{:S(2)}, u32[]{:S(2)}) async-start(bf16[4,8,16,1024]{3,2,1,0:T(8,128)(2,1)} %broadcast_in_dim.16), calls=%async_computation.8 | async-start | bytes 2097152 | tf_op jit(solution)/shard_map/all_to_all | solution.py:17
